TPU v7x, 32 devices: a whole 2x2x4 slice. The times are simulated.
32 devices in a mesh: group: 8 (over z, x), peer: 4 (over y, core).
Axes of the slice: x: 2, y: 2, z: 4, core: 2. Of those that a mesh axis runs over, the one named last changes fastest.
Arguments:
- features: bfloat16 [12288, 1024], P(('group', 'peer')), may hold values from -6 to 6
- task_mask: int32 [12288], P(('group', 'peer')), may hold values from 0 to 65535, as said below
- tower_in: bfloat16 [16, 2048, 1024], P('peer', 'group'), may hold values from -0.1875 to 0.1875
- tower_bias: bfloat16 [16, 2048], P('peer', 'group'), may hold values from -5 to 5
- tower_head: bfloat16 [16, 2048], P('peer', 'group'), may hold values from -0.125 to 0.125
- head_bias: float32 [16], P('peer'), may hold values from -4 to 4
Outputs:
- predictions: float32 [12288, 16], P(('group', 'peer'))
Inputs may be any that keep to these rules, and one draw needn't show every extreme that they name: `task_mask`: only bits 0 to 15 are used. Among the 384 samples of one device (aligned blocks of 384), at most 176 have any one bit set; in every run of 4 blocks that one group holds, some task's bit is set exactly 176 times in each block.
All inputs are finite; a program needn't handle non-finite values.
Results may differ from a plain program's by a relative error of at most 0.0003.
Values may be sent and summed in bfloat16 or wider, within the bound.
A program may use at most 128 MiB of HBM per device.

v0:
```python
import jax
import jax.numpy as jnp
from jax import lax
from jax.sharding import PartitionSpec as P

CAP = 176


def shards(features, task_mask, tower_in, tower_bias, tower_head, head_bias):
    peers = lax.axis_size("peer")
    local_tasks = tower_in.shape[0]
    all_tasks = local_tasks * peers
    task_ids = jnp.arange(all_tasks, dtype=jnp.int32)
    slot_indices = jnp.arange(CAP, dtype=jnp.int32)
    task_bits = task_mask[:, None] >> task_ids[None, :] & 1
    inclusive = jnp.cumsum(task_bits, axis=0)
    slot_rank = inclusive - task_bits
    task_selector = (slot_rank.T[:, None, :] == slot_indices[None, :, None]) & (
        task_bits.T[:, None, :] == 1
    )
    outgoing = jnp.einsum(
        "yra,az->yrz",
        task_selector.astype(jnp.bfloat16),
        features,
        preferred_element_type=jnp.float32,
    ).astype(jnp.bfloat16)
    outgoing = outgoing.reshape(peers, local_tasks, CAP, features.shape[1])
    arrived = lax.all_to_all(outgoing, "peer", split_axis=0, concat_axis=0, tiled=True)
    weight = lax.all_gather(tower_in, "group", axis=1, tiled=True)
    hidden_unit_bias = lax.all_gather(tower_bias, "group", axis=1, tiled=True)
    head_row = lax.all_gather(tower_head, "group", axis=1, tiled=True)
    preact = jnp.einsum("sjcd,jhd->sjch", arrived, weight, preferred_element_type=jnp.float32)
    hidden = jnp.maximum(preact + hidden_unit_bias.astype(jnp.float32)[None, :, None, :], 0.0)
    logits = jnp.einsum(
        "sjch,jh->sjc", hidden, head_row.astype(jnp.float32), precision=lax.Precision.HIGHEST
    )
    logits = logits + head_bias[None, :, None]
    returned_output = lax.all_to_all(
        logits, "peer", split_axis=0, concat_axis=0, tiled=True
    ).reshape(all_tasks, CAP)
    task_selector = (slot_rank.T[:, None, :] == slot_indices[None, :, None]) & (
        task_bits.T[:, None, :] == 1
    )
    return jnp.einsum(
        "ivf,iv->fi",
        task_selector.astype(jnp.float32),
        returned_output,
        precision=lax.Precision.HIGHEST,
    )


def solution(mesh):
    placed = (
        P(("group", "peer"), None),
        P(("group", "peer")),
        P("peer", "group", None),
        P("peer", "group"),
        P("peer", "group"),
        P("peer"),
    )
    return jax.shard_map(
        shards, mesh=mesh, in_specs=placed, out_specs=P(("group", "peer"), None), check_vma=False
    )
```

profile of v0, /device:TPU:0, one launch (start us, length us, event | category | flops | bytes accessed | tf_op | source)
XLA Modules:
  0.0 291.0 jit_solution(16052179998820379908)
XLA Ops:
  6.5 0.0 copy-start
  6.5 0.0 all-gather.2.cloned.1.call-start
  6.5 0.7 all-gather.2.cloned.1.call-update
  7.3 0.7 shift-right-arithmetic_and_fusion.1
  7.9 0.9 reduce-window.6
  8.8 0.2 slice_reduce_fusion
  9.1 0.7 fusion.23
  9.8 0.8 bitcast_subtract_fusion
  10.5 0.0 copy-done
  10.5 4.9 %fusion.14 = bf16[16,176,1024]{2,1,0:T(8,128)(2,1)} fusion(s32[16,384]{1,0:T(8,128)S(1)} %bitcast_subtract_fusion, pred[16,384]{1,0:T(8,128)(4,1)S(1)} %fusion.23, bf16[384,1024]{1,0:T(8,128)(2,1)S(1)} %copy-done), kind=kOutput, calls=%fused_computation.13 | convolution fusion | flops 2219638784 | bytes 6584320 | tf_op jit(solution)/shard_map/yra,az->yrz/dot_general | solution.py:21
  15.4 5.3 %all-to-all-start = ((bf16[4,4,176,1024]{3,2,1,0:T(8,128)(2,1)}), bf16[4,4,176,1024]{3,2,1,0:T(8,128)(2,1)}, u32[]{:S(2)}, u32[]{:S(2)}) async-start(bf16[4,4,176,1024]{3,2,1,0:T(8,128)(2,1)} %bitcast.32), calls=%async_computation | async-start | bytes 11534336 | tf_op jit(solution)/shard_map/all_to_all | solution.py:28
  20.7 0.0 copy-done.1
  20.7 29.4 %all_gather.10 = bf16[4,2048]{1,0:T(4,128)(2,1)S(1)} all-gather(bf16[4,256]{1,0:T(4,128)(2,1)S(1)} %copy-done.1), channel_id=1, replica_groups=mesh['group'=8,'peer'=4] {'group'}, dimensions={1}, use_global_device_ids=true | all-gather | bytes 18432 | tf_op jit(solution)/shard_map/all_gather | solution.py:30
  50.2 0.0 copy-done.2
  50.2 27.3 %all_gather.11 = bf16[4,2048]{1,0:T(4,128)(2,1)S(1)} all-gather(bf16[4,256]{1,0:T(4,128)(2,1)S(1)} %copy-done.2), channel_id=1, replica_groups=mesh['group'=8,'peer'=4] {'group'}, dimensions={1}, use_global_device_ids=true | all-gather | bytes 18432 | tf_op jit(solution)/shard_map/all_gather | solution.py:31
  77.5 9.2 %all-to-all-done = bf16[4,4,176,1024]{3,2,1,0:T(8,128)(2,1)} async-done(((bf16[4,4,176,1024]{3,2,1,0:T(8,128)(2,1)}), bf16[4,4,176,1024]{3,2,1,0:T(8,128)(2,1)}, u32[]{:S(2)}, u32[]{:S(2)}) %all-to-all-start) | async-done | bytes 5767200 | tf_op jit(solution)/shard_map/all_to_all | solution.py:28
  86.7 153.3 %all-gather.2.cloned.1.call-done = bf16[4,2048,1024]{2,1,0:T(8,128)(2,1)} async-done(((bf16[4,256,1024]{2,1,0:T(8,128)(2,1)}), bf16[4,2048,1024]{2,1,0:T(8,128)(2,1)}) %all-gather.2.cloned.1.call-update) | async-done | bytes 16777232 | tf_op jit(solution)/shard_map/all_gather | solution.py:29
  240.0 20.6 %fusion.4 = f32[4,4,176,2048]{3,2,1,0:T(8,128)} fusion(bf16[4,2048,1024]{2,1,0:T(8,128)(2,1)} %all-gather.2.cloned.1.call-done, bf16[4,4,176,1024]{3,2,1,0:T(8,128)(2,1)} %all-to-all-done), kind=kOutput, calls=%fused_computation.4 | convolution fusion | flops 11811160064 | bytes 45613056 | tf_op jit(solution)/shard_map/sjcd,jhd->sjch/dot_general | solution.py:32
  260.6 14.7 %fusion = f32[4,1,4,176]{3,1,2,0:T(1,128)S(1)} fusion(f32[4,4,176,2048]{3,2,1,0:T(8,128)} %fusion.4, f32[4,2048]{1,0:T(4,128)S(1)} %convert_element_type.10, bf16[4,2048,1,1]{1,0,2,3:T(4,128)(2,1)S(1)} %bitcast.33), kind=kOutput, calls=%fused_computation | convolution fusion | flops 80740352 | bytes 23129088 | tf_op jit(solution)/shard_map/sjch,jh->sjc/dot_general | solution.py:34
  275.3 0.0 copy-done.3
  275.3 0.1 fusion.24
  275.4 6.4 %all_to_all.10 = f32[4,4,176]{2,1,0:T(4,128)S(1)} all-to-all(f32[4,4,176]{2,1,0:T(4,128)S(1)} %fusion.24), channel_id=1, replica_groups=mesh['group'=8,'peer'=4] {'peer'}, dimensions={0} | all-to-all | bytes 22528 | tf_op jit(solution)/shard_map/all_to_all | solution.py:38
  281.8 1.8 fusion.10
  283.6 0.6 copy.22
  (6 shorter events, 0.1 us)
Async XLA Ops:
  6.5 4.0 %copy-start = (bf16[384,1024]{1,0:T(8,128)(2,1)S(1)}, bf16[384,1024]{1,0:T(8,128)(2,1)}, u32[]{:S(2)}) copy-start(bf16[384,1024]{1,0:T(8,128)(2,1)} %param.6) | copy-start | bytes 2359300
  6.5 233.5 %all-gather.2.cloned.1.call-start = ((), (), s32[]{:S(2)}) async-start(), calls=%async_computation.2 | async-start | bytes 18874368 | tf_op jit(solution)/shard_map/all_gather | solution.py:29
  15.4 5.3 %copy-start.1 = (bf16[4,256]{1,0:T(4,128)(2,1)S(1)}, bf16[4,256]{1,0:T(4,128)(2,1)}, u32[]{:S(2)}) copy-start(bf16[4,256]{1,0:T(4,128)(2,1)} %param.9) | copy-start | bytes 6148
  15.4 34.7 %copy-start.2 = (bf16[4,256]{1,0:T(4,128)(2,1)S(1)}, bf16[4,256]{1,0:T(4,128)(2,1)}, u32[]{:S(2)}) copy-start(bf16[4,256]{1,0:T(4,128)(2,1)} %param.10) | copy-start | bytes 6148
  15.4 71.2 %all-to-all-start = ((bf16[4,4,176,1024]{3,2,1,0:T(8,128)(2,1)}), bf16[4,4,176,1024]{3,2,1,0:T(8,128)(2,1)}, u32[]{:S(2)}, u32[]{:S(2)}) async-start(bf16[4,4,176,1024]{3,2,1,0:T(8,128)(2,1)} %bitcast.32), calls=%async_computation | async-start | bytes 11534336 | tf_op jit(solution)/shard_map/all_to_all | solution.py:28
  260.6 14.7 %copy-start.3 = (f32[4]{0:T(128)S(1)}, f32[4]{0:T(128)}, u32[]{:S(2)}) copy-start(f32[4]{0:T(128)} %param.11) | copy-start | bytes 52
Sparse Core Ops, SparseCore 0:
  9.5 230.4 all-gather.1
where the time goes:
time: 291 us
  waiting for transfers between devices  163 us (56%)
  blocking collectives  63.1 us (22%)
  matrix products  42 us (14%)
  between operations  13.4 us (5%)
  starting transfers between devices  5.26 us (2%)
  other arithmetic  3.12 us (1%)
    all_gather x1, waiting for transfers between devices, shards(): weight = lax.all_gather(tower_in, 'group', axis=1, tiled=True)  153 us
    all_gather x1, blocking collectives, shards(): hidden_unit_bias = lax.all_gather(tower_bias, 'group', axis=1, tiled=True)  29.4 us
    all_gather x1, blocking collectives, shards(): head_row = lax.all_gather(tower_head, 'group', axis=1, tiled=True)  27.3 us
    dot_general x1, matrix products, shards(): jnp.einsum('sjcd,jhd->sjch', arrived, weight, preferred_element_type=jnp....  20.6 us
    dot_general x1, matrix products, shards(): jnp.einsum('sjch,jh->sjc', hidden, head_row.astype(jnp.float32), precisio...  14.7 us
    all_to_all x1, waiting for transfers between devices, shards(): lax.all_to_all(outgoing, 'peer', split_axis=0, concat_axis=0, tiled=True)  9.23 us
    all_to_all x1, blocking collectives, shards(): lax.all_to_all(logits, 'peer', split_axis=0, concat_axis=0, tiled=True)  6.38 us
  transfers between devices with their start and end apart: 2, of which 2 were waited for; matrix products, arithmetic and copies ran while one was open for 3% of the time, Pallas kernels for 0%

commit v1 on v0

--- a/solution.py
+++ b/solution.py
@@ -28,7 +28,14 @@
     arrived = lax.all_to_all(outgoing, "peer", split_axis=0, concat_axis=0, tiled=True)
     weight = lax.all_gather(tower_in, "group", axis=1, tiled=True)
     hidden_unit_bias = lax.all_gather(tower_bias, "group", axis=1, tiled=True)
-    head_row = lax.all_gather(tower_head, "group", axis=1, tiled=True)
+    ring = [tower_head]
+    for hop in range(7):
+        ring.append(lax.ppermute(ring[-1], "group", [(dev, (dev + 1) % 8) for dev in range(8)]))
+    head_row = jnp.roll(
+        jnp.concatenate(ring[::-1], axis=1),
+        (lax.axis_index("group") + 1) * ring[0].shape[1],
+        axis=1,
+    )
     preact = jnp.einsum("sjcd,jhd->sjch", arrived, weight, preferred_element_type=jnp.float32)
     hidden = jnp.maximum(preact + hidden_unit_bias.astype(jnp.float32)[None, :, None, :], 0.0)
     logits = jnp.einsum(

time: 291 us -> 291 us (level)
  blocking collectives: 63.1 us -> 33.7 us
  waiting for transfers between devices: 163 us -> 189 us
  starting transfers between devices: 5.26 us -> 8.54 us
    ppermute x0 -> x7, waiting for transfers between devices: none -> 37.4 us  [shards(): lax.ppermute(ring[-1], 'group', [(dev, (dev + 1) % 8) for dev in range(8)])]
    all_gather x1 -> x0, blocking collectives: 27.3 us -> none  [shards(): head_row = lax.all_gather(tower_head, 'group', axis=1, tiled=True)]
    all_to_all x1, waiting for transfers between devices: 9.23 us -> 0.01 us  [shards(): lax.all_to_all(outgoing, 'peer', split_axis=0, concat_axis=0, tiled=True)]
    ppermute x0 -> x7, starting transfers between devices: none -> 3.28 us  [shards(): lax.ppermute(ring[-1], 'group', [(dev, (dev + 1) % 8) for dev in range(8)])]
  transfers between devices with their start and end apart: 2 -> 9, of which waited for: 2 -> 7; matrix products, arithmetic and copies ran while one was open for 3% -> 3% of each run, Pallas kernels for 0% -> 0%
where the time goes in v1:
time: 291 us
  waiting for transfers between devices  189 us (65%)
  matrix products  42 us (14%)
  blocking collectives  33.7 us (12%)
  between operations  13.5 us (5%)
  starting transfers between devices  8.54 us (3%)
  other arithmetic  3.12 us (1%)
    all_gather x1, waiting for transfers between devices, shards(): weight = lax.all_gather(tower_in, 'group', axis=1, tiled=True)  151 us
    ppermute x7, waiting for transfers between devices, shards(): lax.ppermute(ring[-1], 'group', [(dev, (dev + 1) % 8) for dev in range(8)])  37.4 us
    all_gather x1, blocking collectives, shards(): hidden_unit_bias = lax.all_gather(tower_bias, 'group', axis=1, tiled=True)  27.4 us
    dot_general x1, matrix products, shards(): jnp.einsum('sjcd,jhd->sjch', arrived, weight, preferred_element_type=jnp....  20.6 us
    dot_general x1, matrix products, shards(): jnp.einsum('sjch,jh->sjc', hidden, head_row.astype(jnp.float32), precisio...  14.7 us
    all_to_all x1, blocking collectives, shards(): lax.all_to_all(logits, 'peer', split_axis=0, concat_axis=0, tiled=True)  6.39 us
  transfers between devices with their start and end apart: 9, of which 7 were waited for; matrix products, arithmetic and copies ran while one was open for 3% of the time, Pallas kernels for 0%

profile of v1, /device:TPU:0, one launch (start us, length us, event | category | flops | bytes accessed | tf_op | source)
XLA Modules:
  0.0 290.9 jit_solution(1731920376847634211)
XLA Ops:
  6.5 0.7 all-gather.2.cloned.1.call-update
  7.3 0.7 shift-right-arithmetic_and_fusion.1
  7.9 0.9 reduce-window.6
  8.8 0.2 slice_reduce_fusion
  9.1 0.7 fusion.23
  9.8 0.8 bitcast_subtract_fusion
  10.5 5.0 %fusion.14 = bf16[16,176,1024]{2,1,0:T(8,128)(2,1)} fusion(s32[16,384]{1,0:T(8,128)S(1)} %bitcast_subtract_fusion, pred[16,384]{1,0:T(8,128)(4,1)S(1)} %fusion.23, bf16[384,1024]{1,0:T(8,128)(2,1)S(1)} %copy-done), kind=kOutput, calls=%fused_computation.13 | convolution fusion | flops 2219638784 | bytes 6584320 | tf_op jit(solution)/shard_map/yra,az->yrz/dot_general | solution.py:21
  15.5 5.3 %all-to-all-start = ((bf16[4,4,176,1024]{3,2,1,0:T(8,128)(2,1)}), bf16[4,4,176,1024]{3,2,1,0:T(8,128)(2,1)}, u32[]{:S(2)}, u32[]{:S(2)}) async-start(bf16[4,4,176,1024]{3,2,1,0:T(8,128)(2,1)} %bitcast.33), calls=%async_computation | async-start | bytes 11534336 | tf_op jit(solution)/shard_map/all_to_all | solution.py:28
  20.8 3.3 %collective-permute-start = (bf16[4,256]{1,0:T(4,128)(2,1)S(1)}, bf16[4,256]{1,0:T(4,128)(2,1)S(1)}, u32[]{:S(2)}, u32[]{:S(2)}) collective-permute-start(bf16[4,256]{1,0:T(4,128)(2,1)S(1)} %copy-done.1), channel_id=1, source_target_pairs={{0,4},{4,8},{8,12},{12,16},{16,20},{20,24},{24,28},{28,0},{1,5},{5... | collective-permute-start | bytes 6152 | tf_op jit(solution)/shard_map/ppermute | solution.py:33
  24.1 4.7 %collective-permute-done = bf16[4,256]{1,0:T(4,128)(2,1)S(1)} collective-permute-done((bf16[4,256]{1,0:T(4,128)(2,1)S(1)}, bf16[4,256]{1,0:T(4,128)(2,1)S(1)}, u32[]{:S(2)}, u32[]{:S(2)}) %collective-permute-start) | collective-permute-done | bytes 2080 | tf_op jit(solution)/shard_map/ppermute | solution.py:33
  28.8 0.0 collective-permute-start.1
  28.8 6.5 %collective-permute-done.1 = bf16[4,256]{1,0:T(4,128)(2,1)S(1)} collective-permute-done((bf16[4,256]{1,0:T(4,128)(2,1)S(1)}, bf16[4,256]{1,0:T(4,128)(2,1)S(1)}, u32[]{:S(2)}, u32[]{:S(2)}) %collective-permute-start.1) | collective-permute-done | bytes 2080 | tf_op jit(solution)/shard_map/ppermute | solution.py:33
  35.3 6.4 %collective-permute-done.2 = bf16[4,256]{1,0:T(4,128)(2,1)S(1)} collective-permute-done((bf16[4,256]{1,0:T(4,128)(2,1)S(1)}, bf16[4,256]{1,0:T(4,128)(2,1)S(1)}, u32[]{:S(2)}, u32[]{:S(2)}) %collective-permute-start.2) | collective-permute-done | bytes 2080 | tf_op jit(solution)/shard_map/ppermute | solution.py:33
  41.7 6.5 %collective-permute-done.3 = bf16[4,256]{1,0:T(4,128)(2,1)S(1)} collective-permute-done((bf16[4,256]{1,0:T(4,128)(2,1)S(1)}, bf16[4,256]{1,0:T(4,128)(2,1)S(1)}, u32[]{:S(2)}, u32[]{:S(2)}) %collective-permute-start.3) | collective-permute-done | bytes 2080 | tf_op jit(solution)/shard_map/ppermute | solution.py:33
  48.3 6.6 %collective-permute-done.4 = bf16[4,256]{1,0:T(4,128)(2,1)S(1)} collective-permute-done((bf16[4,256]{1,0:T(4,128)(2,1)S(1)}, bf16[4,256]{1,0:T(4,128)(2,1)S(1)}, u32[]{:S(2)}, u32[]{:S(2)}) %collective-permute-start.4) | collective-permute-done | bytes 2080 | tf_op jit(solution)/shard_map/ppermute | solution.py:33
  54.9 6.6 %collective-permute-done.5 = bf16[4,256]{1,0:T(4,128)(2,1)S(1)} collective-permute-done((bf16[4,256]{1,0:T(4,128)(2,1)S(1)}, bf16[4,256]{1,0:T(4,128)(2,1)S(1)}, u32[]{:S(2)}, u32[]{:S(2)}) %collective-permute-start.5) | collective-permute-done | bytes 2080 | tf_op jit(solution)/shard_map/ppermute | solution.py:33
  61.5 27.4 %all_gather.7 = bf16[4,2048]{1,0:T(4,128)(2,1)S(1)} all-gather(bf16[4,256]{1,0:T(4,128)(2,1)S(1)} %copy-done.2), channel_id=1, replica_groups=mesh['group'=8,'peer'=4] {'group'}, dimensions={1}, use_global_device_ids=true | all-gather | bytes 18432 | tf_op jit(solution)/shard_map/all_gather | solution.py:30
  89.1 150.8 %all-gather.2.cloned.1.call-done = bf16[4,2048,1024]{2,1,0:T(8,128)(2,1)} async-done(((bf16[4,256,1024]{2,1,0:T(8,128)(2,1)}), bf16[4,2048,1024]{2,1,0:T(8,128)(2,1)}) %all-gather.2.cloned.1.call-update) | async-done | bytes 16777232 | tf_op jit(solution)/shard_map/all_gather | solution.py:29
  239.9 20.6 %fusion.4 = f32[4,4,176,2048]{3,2,1,0:T(8,128)} fusion(bf16[4,2048,1024]{2,1,0:T(8,128)(2,1)} %all-gather.2.cloned.1.call-done, bf16[4,4,176,1024]{3,2,1,0:T(8,128)(2,1)} %all-to-all-done), kind=kOutput, calls=%fused_computation.4 | convolution fusion | flops 11811160064 | bytes 45613056 | tf_op jit(solution)/shard_map/sjcd,jhd->sjch/dot_general | solution.py:39
  260.5 14.7 %fusion = f32[4,1,4,176]{3,1,2,0:T(1,128)S(1)} fusion(f32[4,4,176,2048]{3,2,1,0:T(8,128)} %fusion.4, f32[4,2048]{1,0:T(4,128)S(1)} %convert_element_type.10, bf16[4,2048,1,1]{1,0,2,3:T(4,128)(2,1)S(1)} %dynamic-slice_bitcast_fusion), kind=kOutput, calls=%fused_computation | convolution fusion | flops 80740352 | bytes 23129088 | tf_op jit(solution)/shard_map/sjch,jh->sjc/dot_general | solution.py:41
  275.2 0.1 fusion.24
  275.3 6.4 %all_to_all.10 = f32[4,4,176]{2,1,0:T(4,128)S(1)} all-to-all(f32[4,4,176]{2,1,0:T(4,128)S(1)} %fusion.24), channel_id=1, replica_groups=mesh['group'=8,'peer'=4] {'peer'}, dimensions={0} | all-to-all | bytes 22528 | tf_op jit(solution)/shard_map/all_to_all | solution.py:45
  281.7 1.8 fusion.10
  283.5 0.6 copy.22
  (36 shorter events, 0.3 us)
Async XLA Ops:
  6.5 4.0 %copy-start = (bf16[384,1024]{1,0:T(8,128)(2,1)S(1)}, bf16[384,1024]{1,0:T(8,128)(2,1)}, u32[]{:S(2)}) copy-start(bf16[384,1024]{1,0:T(8,128)(2,1)} %param.6) | copy-start | bytes 2359300
  6.5 233.4 %all-gather.2.cloned.1.call-start = ((), (), s32[]{:S(2)}) async-start(), calls=%async_computation.2 | async-start | bytes 18874368 | tf_op jit(solution)/shard_map/all_gather | solution.py:29
  15.5 5.3 %copy-start.1 = (bf16[4,256]{1,0:T(4,128)(2,1)S(1)}, bf16[4,256]{1,0:T(4,128)(2,1)}, u32[]{:S(2)}) copy-start(bf16[4,256]{1,0:T(4,128)(2,1)} %param.10) | copy-start | bytes 6148
  15.5 46.0 %copy-start.2 = (bf16[4,256]{1,0:T(4,128)(2,1)S(1)}, bf16[4,256]{1,0:T(4,128)(2,1)}, u32[]{:S(2)}) copy-start(bf16[4,256]{1,0:T(4,128)(2,1)} %param.9) | copy-start | bytes 6148
  15.5 73.6 %all-to-all-start = ((bf16[4,4,176,1024]{3,2,1,0:T(8,128)(2,1)}), bf16[4,4,176,1024]{3,2,1,0:T(8,128)(2,1)}, u32[]{:S(2)}, u32[]{:S(2)}) async-start(bf16[4,4,176,1024]{3,2,1,0:T(8,128)(2,1)} %bitcast.33), calls=%async_computation | async-start | bytes 11534336 | tf_op jit(solution)/shard_map/all_to_all | solution.py:28
  20.8 8.0 %collective-permute-start = (bf16[4,256]{1,0:T(4,128)(2,1)S(1)}, bf16[4,256]{1,0:T(4,128)(2,1)S(1)}, u32[]{:S(2)}, u32[]{:S(2)}) collective-permute-start(bf16[4,256]{1,0:T(4,128)(2,1)S(1)} %copy-done.1), channel_id=1, source_target_pairs={{0,4},{4,8},{8,12},{12,16},{16,20},{20,24},{24,28},{28,0},{1,5},{5... | collective-permute-start | bytes 6152 | tf_op jit(solution)/shard_map/ppermute | solution.py:33
  28.8 6.5 %collective-permute-start.1 = (bf16[4,256]{1,0:T(4,128)(2,1)S(1)}, bf16[4,256]{1,0:T(4,128)(2,1)S(1)}, u32[]{:S(2)}, u32[]{:S(2)}) collective-permute-start(bf16[4,256]{1,0:T(4,128)(2,1)S(1)} %collective-permute-done), channel_id=1, source_target_pairs={{0,4},{4,8},{8,12},{12,16},{16,20},{20,24},{24,28},{28,0},{1,5},{5... | collective-permute-start | bytes 6152 | tf_op jit(solution)/shard_map/ppermute | solution.py:33
  35.3 6.5 %collective-permute-start.2 = (bf16[4,256]{1,0:T(4,128)(2,1)S(1)}, bf16[4,256]{1,0:T(4,128)(2,1)S(1)}, u32[]{:S(2)}, u32[]{:S(2)}) collective-permute-start(bf16[4,256]{1,0:T(4,128)(2,1)S(1)} %collective-permute-done.1), channel_id=1, source_target_pairs={{0,4},{4,8},{8,12},{12,16},{16,20},{20,24},{24,28},{28,0},{1,5},{5... | collective-permute-start | bytes 6152 | tf_op jit(solution)/shard_map/ppermute | solution.py:33
  41.7 6.5 %collective-permute-start.3 = (bf16[4,256]{1,0:T(4,128)(2,1)S(1)}, bf16[4,256]{1,0:T(4,128)(2,1)S(1)}, u32[]{:S(2)}, u32[]{:S(2)}) collective-permute-start(bf16[4,256]{1,0:T(4,128)(2,1)S(1)} %collective-permute-done.2), channel_id=1, source_target_pairs={{0,4},{4,8},{8,12},{12,16},{16,20},{20,24},{24,28},{28,0},{1,5},{5... | collective-permute-start | bytes 6152 | tf_op jit(solution)/shard_map/ppermute | solution.py:33
  48.3 6.6 %collective-permute-start.4 = (bf16[4,256]{1,0:T(4,128)(2,1)S(1)}, bf16[4,256]{1,0:T(4,128)(2,1)S(1)}, u32[]{:S(2)}, u32[]{:S(2)}) collective-permute-start(bf16[4,256]{1,0:T(4,128)(2,1)S(1)} %collective-permute-done.3), channel_id=1, source_target_pairs={{0,4},{4,8},{8,12},{12,16},{16,20},{20,24},{24,28},{28,0},{1,5},{5... | collective-permute-start | bytes 6152 | tf_op jit(solution)/shard_map/ppermute | solution.py:33
  54.9 6.6 %collective-permute-start.5 = (bf16[4,256]{1,0:T(4,128)(2,1)S(1)}, bf16[4,256]{1,0:T(4,128)(2,1)S(1)}, u32[]{:S(2)}, u32[]{:S(2)}) collective-permute-start(bf16[4,256]{1,0:T(4,128)(2,1)S(1)} %collective-permute-done.4), channel_id=1, source_target_pairs={{0,4},{4,8},{8,12},{12,16},{16,20},{20,24},{24,28},{28,0},{1,5},{5... | collective-permute-start | bytes 6152 | tf_op jit(solution)/shard_map/ppermute | solution.py:33
  61.5 27.4 %collective-permute-start.6 = (bf16[4,256]{1,0:T(4,128)(2,1)S(1)}, bf16[4,256]{1,0:T(4,128)(2,1)S(1)}, u32[]{:S(2)}, u32[]{:S(2)}) collective-permute-start(bf16[4,256]{1,0:T(4,128)(2,1)S(1)} %collective-permute-done.5), channel_id=1, source_target_pairs={{0,4},{4,8},{8,12},{12,16},{16,20},{20,24},{24,28},{28,0},{1,5},{5... | collective-permute-start | bytes 6152 | tf_op jit(solution)/shard_map/ppermute | solution.py:33
  260.5 14.7 %copy-start.3 = (f32[4]{0:T(128)S(1)}, f32[4]{0:T(128)}, u32[]{:S(2)}) copy-start(f32[4]{0:T(128)} %param.11) | copy-start | bytes 52
Sparse Core Ops, SparseCore 0:
  9.5 230.3 all-gather.1
